TPU v7x, 32 devices: a whole 2x2x4 slice. The times are simulated.
32 devices in a mesh: dp: 4 (over x, core), fsdp: 2 (over y), tensor: 4 (over z).
Axes of the slice: x: 2, y: 2, z: 4, core: 2. Of those that a mesh axis runs over, the one named last changes fastest.
Arguments:
- tokens: bfloat16 [8, 768, 8192], P(('dp', 'fsdp'), 'tensor'), may hold values from -6 to 6
- norm_gain: float32 [8192], replicated, may hold values from 0.85 to 4
- w_qkv: bfloat16 [8192, 5120], P(('dp', 'fsdp'), 'tensor'), may hold values from -0.3 to 0.3
- a_query: bfloat16 [8192, 16], replicated, may hold values from -0.0625 to 0.0625
- query_up_adapter: bfloat16 [16, 4096], P(None, 'tensor'), may hold values from -1.5 to 1.5
- a_value: bfloat16 [8192, 16], replicated, may hold values from -0.0625 to 0.0625
- value_up_adapter: bfloat16 [16, 512], P(None, 'tensor'), may hold values from -1.5 to 1.5
- out_grad: bfloat16 [8, 768, 4096], P(('dp', 'fsdp'), 'tensor'), may hold values from -6 to 6
Outputs:
- attn_out: bfloat16 [8, 768, 4096], P(('dp', 'fsdp'), 'tensor')
- grad_a_query: float32 [8192, 16], replicated
- grad_b_query: float32 [16, 4096], P(None, 'tensor')
- grad_a_value: float32 [8192, 16], replicated
- grad_b_value: float32 [16, 512], P(None, 'tensor')
All inputs are finite; a program needn't handle non-finite values.
Results may differ from a plain program's by a relative error of at most 0.015.
The roundings to bfloat16 on the way count: a program that leaves them out, or rounds other values in their place, can miss the bound.
Values may be sent and summed in bfloat16 or wider, within the bound.
A program may use at most 256 MiB of HBM per device.

v0:
```python
import math
import jax
import jax.numpy as jnp
from jax import lax
from jax.sharding import PartitionSpec as P

HD = 128
QUERY_PER_KV = 8
EPSILON = 1e-05
ADAPTER_SCALE = 2.0
ROPE_BASE = 500000.0


def normalize(own_rows, norm_gain):
    widened = own_rows.astype(jnp.float32)
    mean_square = jnp.mean(widened * widened, axis=-1, keepdims=True)
    return (widened * lax.rsqrt(mean_square + EPSILON) * norm_gain).astype(jnp.bfloat16)


def rotary(heads_block):
    sequence_length = heads_block.shape[0]
    half_dim = heads_block.shape[-1] // 2
    positions = jnp.arange(sequence_length, dtype=jnp.float32)[:, None]
    inv_freq = ROPE_BASE ** (-jnp.arange(half_dim, dtype=jnp.float32) / half_dim)
    angles = positions * inv_freq
    cosine = jnp.cos(angles)[:, None, :]
    sine_table = jnp.sin(angles)[:, None, :]
    front_half = heads_block[..., :half_dim].astype(jnp.float32)
    back_half = heads_block[..., half_dim:].astype(jnp.float32)
    turned = jnp.concatenate(
        [
            front_half * cosine - back_half * sine_table,
            back_half * cosine + front_half * sine_table,
        ],
        -1,
    )
    return turned.astype(jnp.bfloat16)


def attend(query_rows, key_heads, value_rows):
    sequence_length = query_rows.shape[0]
    kv_heads = key_heads.shape[1] // HD
    rot_queries = rotary(query_rows.reshape(sequence_length, kv_heads * QUERY_PER_KV, HD))
    rot_keys = rotary(key_heads.reshape(sequence_length, kv_heads, HD))
    split_values = value_rows.reshape(sequence_length, kv_heads, HD)
    causal = jnp.arange(sequence_length)[:, None] >= jnp.arange(sequence_length)[None, :]

    def one_head(head_index):
        q_head = lax.dynamic_index_in_dim(rot_queries, head_index, 1, keepdims=False)
        k_head = lax.dynamic_index_in_dim(rot_keys, head_index // QUERY_PER_KV, 1, keepdims=False)
        v_head = lax.dynamic_index_in_dim(
            split_values, head_index // QUERY_PER_KV, 1, keepdims=False
        )
        scores = jnp.dot(q_head, k_head.T, preferred_element_type=jnp.float32) * (
            1.0 / math.sqrt(HD)
        )
        scores = jnp.where(causal, scores, -1e30)
        row_max = jnp.max(scores, axis=-1, keepdims=True)
        weights = jnp.exp(scores - row_max)
        probabilities = (weights / jnp.sum(weights, axis=-1, keepdims=True)).astype(jnp.bfloat16)
        return jnp.dot(probabilities, v_head, preferred_element_type=jnp.float32).astype(
            jnp.bfloat16
        )

    per_head = lax.map(one_head, jnp.arange(kv_heads * QUERY_PER_KV, dtype=jnp.int32))
    return jnp.transpose(per_head, (1, 0, 2)).reshape(sequence_length, kv_heads * QUERY_PER_KV * HD)


def local(tokens, norm_gain, w_qkv, a_query, query_up_adapter, a_value, value_up_adapter, out_grad):
    normed_input = normalize(tokens[0], norm_gain)
    gathered = lax.all_gather(normed_input, "tensor", axis=0, tiled=True)
    sequence_length = gathered.shape[0]
    col_count = w_qkv.shape[1]
    projected = jnp.dot(
        gathered,
        lax.all_gather(w_qkv, ("dp", "fsdp"), axis=0, tiled=True),
        preferred_element_type=jnp.float32,
    )
    narrow_rank_rows = a_query.shape[1]
    down_projected = jnp.dot(
        gathered, jnp.concatenate([a_query, a_value], 1), preferred_element_type=jnp.float32
    ).astype(jnp.bfloat16)
    kv_local = col_count // ((QUERY_PER_KV + 2) * HD)
    grouped_queries = projected.reshape(sequence_length, kv_local, QUERY_PER_KV + 2, HD)
    query_rows = (
        grouped_queries[:, :, :QUERY_PER_KV].reshape(sequence_length, -1)
        + ADAPTER_SCALE
        * jnp.dot(
            down_projected[:, :narrow_rank_rows],
            query_up_adapter,
            preferred_element_type=jnp.float32,
        )
    ).astype(jnp.bfloat16)
    key_heads = (
        grouped_queries[:, :, QUERY_PER_KV].reshape(sequence_length, -1).astype(jnp.bfloat16)
    )
    value_rows = (
        grouped_queries[:, :, QUERY_PER_KV + 1].reshape(sequence_length, -1)
        + ADAPTER_SCALE
        * jnp.dot(
            down_projected[:, narrow_rank_rows:],
            value_up_adapter,
            preferred_element_type=jnp.float32,
        )
    ).astype(jnp.bfloat16)
    grad_rows = lax.all_to_all(out_grad[0], "tensor", split_axis=1, concat_axis=0, tiled=True)
    attended, pullback = jax.vjp(attend, query_rows, key_heads, value_rows)
    query_gradient, grad_keys, value_gradient = pullback(grad_rows)
    out_rows = lax.all_to_all(attended, "tensor", split_axis=0, concat_axis=1, tiled=True)
    query_up_gradient = ADAPTER_SCALE * jnp.einsum(
        "fb,fd->bd",
        down_projected[:, :narrow_rank_rows],
        query_gradient,
        preferred_element_type=jnp.float32,
    )
    value_up_gradient = ADAPTER_SCALE * jnp.einsum(
        "fb,fd->bd",
        down_projected[:, narrow_rank_rows:],
        value_gradient,
        preferred_element_type=jnp.float32,
    )
    middle_gradient = jnp.concatenate(
        [
            jnp.dot(query_gradient, query_up_adapter.T, preferred_element_type=jnp.float32),
            jnp.dot(value_gradient, value_up_adapter.T, preferred_element_type=jnp.float32),
        ],
        1,
    )
    mid_summed = lax.psum(middle_gradient, "tensor").astype(jnp.bfloat16)
    down_gradient = ADAPTER_SCALE * jnp.einsum(
        "uh,ux->hx", gathered, mid_summed, preferred_element_type=jnp.float32
    )
    down_gradient, query_up_gradient, value_up_gradient = lax.psum(
        (down_gradient, query_up_gradient, value_up_gradient), ("dp", "fsdp")
    )
    return (
        out_rows[None],
        down_gradient[:, :narrow_rank_rows],
        query_up_gradient,
        down_gradient[:, narrow_rank_rows:],
        value_up_gradient,
    )


def solution(mesh):
    return jax.shard_map(
        local,
        mesh=mesh,
        in_specs=(
            P(("dp", "fsdp"), "tensor", None),
            P(),
            P(("dp", "fsdp"), "tensor"),
            P(),
            P(None, "tensor"),
            P(),
            P(None, "tensor"),
            P(("dp", "fsdp"), "tensor", None),
        ),
        out_specs=(
            P(("dp", "fsdp"), "tensor", None),
            P(),
            P(None, "tensor"),
            P(),
            P(None, "tensor"),
        ),
        check_vma=False,
    )
```

profile of v0, /device:TPU:0, one launch (start us, length us, event | category | flops | bytes accessed | tf_op | source)
XLA Modules:
  0.0 691.3 jit_solution(7818503089707505698)
XLA Ops:
  7.2 2.8 fusion.62
  10.0 3.3 fusion.64
  17.5 6.3 all-to-all-start.1
  25.4 77.7 %all-to-all-done.1 = bf16[192,4,1024]{2,0,1:T(8,128)(2,1)S(1)} async-done(((bf16[192,4,1024]{2,0,1:T(8,128)(2,1)}), bf16[192,4,1024]{2,0,1:T(8,128)(2,1)S(1)}, u32[]{:S(2)}, u32[]{:S(2)}) %all-to-all-start.1) | async-done | bytes 1572896 | tf_op jit(solution)/shard_map/all_to_all | solution.py:106
  105.0 158.8 %all-gather.3.cloned.1.call-done = bf16[768,8192]{1,0:T(8,128)(2,1)} async-done(((bf16[192,8192]{1,0:T(8,128)(2,1)}), bf16[768,8192]{1,0:T(8,128)(2,1)}) %all-gather.3.cloned.1.call-update) | async-done | bytes 12582928 | tf_op jit(solution)/shard_map/all_gather | solution.py:71
  263.8 8.4 %convolution_convert_fusion.2 = bf16[768,32]{0,1:T(8,128)(2,1)S(1)} fusion(bf16[768,8192]{1,0:T(8,128)(2,1)} %all-gather.3.cloned.1.call-done, bf16[8192,16]{0,1:T(8,128)(2,1)S(1)} %copy-done.6, bf16[8192,16]{0,1:T(8,128)(2,1)S(1)} %copy-done.7), kind=kOutput, calls=%fused_computation.94 | convolution fusion | flops 403726336 | bytes 13156352 | tf_op jit(solution)/shard_map/dot_general | solution.py:80
  272.2 100.1 %all-gather.5.cloned.1.call-done = bf16[8192,1280]{1,0:T(8,128)(2,1)} async-done(((bf16[1024,1280]{1,0:T(8,128)(2,1)}), bf16[8192,1280]{1,0:T(8,128)(2,1)}) %all-gather.5.cloned.1.call-update) | async-done | bytes 20971536 | tf_op jit(solution)/shard_map/all_gather | solution.py:76
  372.3 22.9 %fusion.95 = f32[768,1280]{0,1:T(8,128)S(1)} fusion(bf16[768,8192]{1,0:T(8,128)(2,1)} %all-gather.3.cloned.1.call-done, bf16[8192,1280]{1,0:T(8,128)(2,1)} %all-gather.5.cloned.1.call-done), kind=kOutput, calls=%fused_computation.131 | convolution fusion | flops 16106127360 | bytes 37486592 | tf_op jit(solution)/shard_map/dot_general | solution.py:74
  407.8 85.5 %while.52 = (s32[]{:T(128)}, bf16[8,768,128]{2,1,0:T(8,128)(2,1)}, s32[8]{0:T(128)S(1)}, bf16[8,128,768]{2,1,0:T(8,128)(2,1)}, f32[8,768,768]{1,2,0:T(8,128)}, /...) while((s32[]{:T(128)}, bf16[8,768,128]{2,1,0:T(8,128)(2,1)}, ...), condition=%wide.region_5.6_spmd.clone, body=%wide.region_1.5_spmd.clone.sunk | while | flops 310344960 | bytes 20494060 | solution.py:65
  465.1 2.6 fusion.126
  493.5 98.7 %while.53 = (s32[]{:T(128)}, bf16[768,8,128]{0,2,1:T(8,128)(2,1)S(1)}, bf16[768,1,128]{2,0,1:T(8,128)(2,1)}, s32[8]{0:T(128)S(1)}, bf16[8,768,128]{2,1,0:T(8,128...) while((s32[]{:T(128)}, ...), condition=%wide.region_9.10_spmd.clone, body=%wide.region_6.9_spmd.clone.sunk | while | flops 464683776 | bytes 17364168 | solution.py:65
  499.7 3.0 fusion.133
  511.9 3.0 fusion.133
  524.3 3.0 fusion.133
  536.6 3.0 fusion.133
  548.9 3.0 fusion.133
  561.2 3.0 fusion.133
  573.5 3.0 fusion.133
  585.9 3.0 fusion.133
  595.4 20.2 %psum.28 = bf16[768,32]{0,1:T(8,128)(2,1)S(1)} all-reduce(f32[768,32]{0,1:T(8,128)S(1)} %pad_maximum_fusion.2), channel_id=1, replica_groups=mesh['dp'=4,'fsdp'=2,'tensor'=4] {'tensor'}, use_global_device_ids=true, to_apply=%region_10.11 | all-reduce | flops 24576 | bytes 147456 | tf_op jit(solution)/shard_map/psum | solution.py:129
  615.6 7.9 %convolution_multiply_fusion = f32[8192,32]{0,1:T(8,128)} fusion(bf16[768,8192]{1,0:T(8,128)(2,1)} %all-gather.3.cloned.1.call-done, bf16[768,32]{0,1:T(8,128)(2,1)S(1)} %psum.28), kind=kOutput, calls=%fused_computation.71 | convolution fusion | flops 402915328 | bytes 13680640 | tf_op jit(solution)/shard_map/uh,ux->hx/dot_general | solution.py:130
  626.7 3.6 all-to-all-start
  630.4 13.6 %psum.31 = f32[16,128]{1,0:T(8,128)} all-reduce(f32[16,128]{1,0:T(8,128)S(1)} %convolution_multiply_fusion.3), channel_id=1, replica_groups=mesh['dp'=4,'fsdp'=2,'tensor'=4] {'dp','fsdp'}, use_global_device_ids=true, to_apply=%region_13.14 | all-reduce | flops 2048 | bytes 16384 | tf_op jit(solution)/shard_map/psum | solution.py:133
  644.0 34.3 %all-reduce.5.cloned.1.call-done = (f32[8192,32]{0,1:T(8,128)}, f32[16,1024]{1,0:T(8,128)}) async-done(((f32[8192,32]{0,1:T(8,128)}, f32[16,1024]{1,0:T(8,128)}), (f32[8192,32]{0,1:T(8,128)}, f32[16,1024]{1,0:T(8,128)})) %all-reduce.5.cloned.1.call-update) | async-done | bytes 1114128 | tf_op jit(solution)/shard_map/psum | solution.py:133
  (264 shorter events, 174.3 us)
Async XLA Ops:
  7.2 392.2 %copy-start = (bf16[16,1024]{1,0:T(8,128)(2,1)S(1)}, bf16[16,1024]{1,0:T(8,128)(2,1)}, u32[]{:S(2)}) copy-start(bf16[16,1024]{1,0:T(8,128)(2,1)} %param.16) | copy-start | bytes 98308
  7.2 2.8 copy-start.1
  7.2 256.6 %all-gather.3.cloned.1.call-start = ((), (), s32[]{:S(2)}) async-start(), calls=%async_computation.2 | async-start | bytes 15728640 | tf_op jit(solution)/shard_map/all_gather | solution.py:71
  13.3 1.4 copy-start.3
  13.3 359.0 %all-gather.5.cloned.1.call-start = ((), (), s32[]{:S(2)}) async-start(), calls=%async_computation.3 | async-start | bytes 23592960 | tf_op jit(solution)/shard_map/all_gather | solution.py:76
  17.5 85.6 %all-to-all-start.1 = ((bf16[192,4,1024]{2,0,1:T(8,128)(2,1)}), bf16[192,4,1024]{2,0,1:T(8,128)(2,1)S(1)}, u32[]{:S(2)}, u32[]{:S(2)}) async-start(bf16[192,4,1024]{2,0,1:T(8,128)(2,1)} %copy.38), calls=%async_computation.1 | async-start | bytes 3145728 | tf_op jit(solution)/shard_map/all_to_all | solution.py:106
  23.9 654.4 %all-reduce.5.cloned.1.call-start = ((), (), s32[]{:S(2)}) async-start(), calls=%async_computation.4 | async-start | bytes 2228224 | tf_op jit(solution)/shard_map/psum | solution.py:133
  103.6 160.3 %copy-start.6 = (bf16[8192,16]{0,1:T(8,128)(2,1)S(1)}, bf16[8192,16]{0,1:T(8,128)(2,1)}, u32[]{:S(2)}) copy-start(bf16[8192,16]{0,1:T(8,128)(2,1)} %param.17) | copy-start | bytes 786436
  103.6 160.2 %copy-start.7 = (bf16[8192,16]{0,1:T(8,128)(2,1)S(1)}, bf16[8192,16]{0,1:T(8,128)(2,1)}, u32[]{:S(2)}) copy-start(bf16[8192,16]{0,1:T(8,128)(2,1)} %param.15) | copy-start | bytes 786436
  406.9 0.7 copy-start.9
  592.2 0.9 copy-start.2
  593.7 1.5 copy-start.5
  615.6 8.0 %copy-start.4 = (bf16[8,768,128]{2,1,0:T(8,128)(2,1)S(1)}, bf16[8,768,128]{2,1,0:T(8,128)(2,1)}, u32[]{:S(2)}) copy-start(bf16[8,768,128]{2,1,0:T(8,128)(2,1)} %get-tuple-element.648) | copy-start | bytes 4718596
  626.7 53.8 %all-to-all-start = ((bf16[4,192,1024]{2,1,0:T(8,128)(2,1)}), bf16[4,192,1024]{2,1,0:T(8,128)(2,1)S(1)}, u32[]{:S(2)}, u32[]{:S(2)}) async-start(bf16[4,192,1024]{2,1,0:T(8,128)(2,1)} %all_to_all.24), calls=%async_computation | async-start | bytes 3145728 | tf_op jit(solution)/shard_map/all_to_all | solution.py:109
  681.7 2.4 copy-start.8
Sparse Core Ops, SparseCore 0:
  13.4 250.3 all-gather.2
  265.7 106.5 all-gather.4
  623.7 54.5 all-reduce.4
where the time goes:
time: 693 us; the launch traced here: 691 us
  waiting for transfers between devices  372 us (54%)
  matrix products  121 us (17%)
  other arithmetic  66.7 us (10%)
  local copies, waits for them, and re-layouts  57.7 us (8%)
  blocking collectives  33.8 us (5%)
  loops' own time  16.5 us (2%)
  between operations  14.1 us (2%)
  starting transfers between devices  9.99 us (1%)
    all_gather x1, waiting for transfers between devices, local(): gathered = lax.all_gather(normed_input, 'tensor', axis=0, tiled=True)  159 us
    all_gather x1, waiting for transfers between devices, local(): lax.all_gather(w_qkv, ('dp', 'fsdp'), axis=0, tiled=True)  100 us
    all_to_all x1, waiting for transfers between devices, local(): lax.all_to_all(out_grad[0], 'tensor', split_axis=1, concat_axis=0, tiled=...  77.7 us
    dot_general x24, matrix products, one_head(): jnp.dot(probabilities, v_head, preferred_element_type=jnp.float32)  48.5 us
    psum x1, waiting for transfers between devices, local(): lax.psum((down_gradient, query_up_gradient, value_up_gradient), ('dp', 'f...  34.3 us
    dynamic_update_slice x24, other arithmetic, attend(): lax.map(one_head, jnp.arange(kv_heads * QUERY_PER_KV, dtype=jnp.int32))  31.9 us
    dot_general x16, matrix products, one_head(): jnp.dot(q_head, k_head.T, preferred_element_type=jnp.float32)  28.8 us
    dot_general x1, matrix products, local(): jnp.dot(gathered, lax.all_gather(w_qkv, ('dp', 'fsdp'), axis=0, tiled=Tru...  22.9 us
  transfers between devices with their start and end apart: 5, of which 4 were waited for; matrix products, arithmetic and copies ran while one was open for 2% of the time, Pallas kernels for 0%

commit v1 on v0

--- a/solution.py
+++ b/solution.py
@@ -9,6 +9,17 @@
 EPSILON = 1e-05
 ADAPTER_SCALE = 2.0
 ROPE_BASE = 500000.0
+
+
+def pass_along(block, axis, dim):
+    size = lax.axis_size(axis)
+    route = [(i, (i + 1) % size) for i in range(size)]
+    parts = [block]
+    for reach in range(1, size):
+        parts = [lax.ppermute(parts[0], axis, route), *parts]
+    whole = jnp.concatenate(parts, axis=dim)
+    shift = (lax.axis_index(axis) + 1) * parts[-1].shape[dim]
+    return jnp.roll(whole, shift, axis=dim)
 
 
 def normalize(own_rows, norm_gain):
@@ -68,7 +79,7 @@
 
 def local(tokens, norm_gain, w_qkv, a_query, query_up_adapter, a_value, value_up_adapter, out_grad):
     normed_input = normalize(tokens[0], norm_gain)
-    gathered = lax.all_gather(normed_input, "tensor", axis=0, tiled=True)
+    gathered = pass_along(normed_input, "tensor", 0)
     sequence_length = gathered.shape[0]
     col_count = w_qkv.shape[1]
     projected = jnp.dot(

time: 693 us -> 624 us (0.900)
  waiting for transfers between devices: 372 us -> 268 us
  local copies, waits for them, and re-layouts: 57.7 us -> 88.6 us
    all_gather x1 -> x0, waiting for transfers between devices: 159 us -> none  [local(): gathered = lax.all_gather(normed_input, 'tensor', axis=0, tiled=True)]
    ppermute x0 -> x3, waiting for transfers between devices: none -> 141 us  [pass_along(): parts = [lax.ppermute(parts[0], axis, route), *parts]]
    all_gather x1, waiting for transfers between devices: 100 us -> 0.02 us  [local(): lax.all_gather(w_qkv, ('dp', 'fsdp'), axis=0, tiled=True)]
    unnamed x24 -> x38, local copies, waits for them, and re-layouts: 5.55 us -> 26 us
    all_to_all x1, waiting for transfers between devices: 77.7 us -> 90.7 us  [local(): lax.all_to_all(out_grad[0], 'tensor', split_axis=1, concat_axis=0, tiled=...]
  transfers between devices with their start and end apart: 5 -> 7, of which waited for: 4 -> 4; matrix products, arithmetic and copies ran while one was open for 2% -> 5% of each run, Pallas kernels for 0% -> 0%
where the time goes in v1:
time: 624 us; the launch traced here: 622 us
  waiting for transfers between devices  268 us (43%)
  matrix products  120 us (19%)
  local copies, waits for them, and re-layouts  88.6 us (14%)
  other arithmetic  70.8 us (11%)
  blocking collectives  31.4 us (5%)
  loops' own time  16.5 us (3%)
  between operations  14.5 us (2%)
  starting transfers between devices  11.8 us (2%)
    ppermute x3, waiting for transfers between devices, pass_along(): parts = [lax.ppermute(parts[0], axis, route), *parts]  141 us
    all_to_all x1, waiting for transfers between devices, local(): lax.all_to_all(out_grad[0], 'tensor', split_axis=1, concat_axis=0, tiled=...  90.7 us
    dot_general x24, matrix products, one_head(): jnp.dot(probabilities, v_head, preferred_element_type=jnp.float32)  48.7 us
    dynamic_update_slice x24, other arithmetic, attend(): lax.map(one_head, jnp.arange(kv_heads * QUERY_PER_KV, dtype=jnp.int32))  36.6 us
    psum x1, waiting for transfers between devices, local(): lax.psum((down_gradient, query_up_gradient, value_up_gradient), ('dp', 'f...  35.4 us
    dot_general x16, matrix products, one_head(): jnp.dot(q_head, k_head.T, preferred_element_type=jnp.float32)  28.8 us
    unnamed x38, local copies, waits for them, and re-layouts  26 us
    dot_general x1, matrix products, local(): jnp.dot(gathered, lax.all_gather(w_qkv, ('dp', 'fsdp'), axis=0, tiled=Tru...  23.2 us
  transfers between devices with their start and end apart: 7, of which 4 were waited for; matrix products, arithmetic and copies ran while one was open for 5% of the time, Pallas kernels for 0%

profile of v1, /device:TPU:0, one launch (start us, length us, event | category | flops | bytes accessed | tf_op | source)
XLA Modules:
  0.0 622.2 jit_solution(341606417384879904)
XLA Ops:
  11.6 3.1 collective-permute-start
  14.7 70.1 %collective-permute-done = bf16[192,8192]{1,0:T(8,128)(2,1)S(1)} collective-permute-done((bf16[192,8192]{1,0:T(8,128)(2,1)S(1)}, bf16[192,8192]{1,0:T(8,128)(2,1)S(1)}, u32[]{:S(2)}, u32[]{:S(2)}) %collective-permute-start) | collective-permute-done | bytes 3145760 | tf_op jit(solution)/shard_map/ppermute | solution.py:19
  86.6 71.2 %collective-permute-done.1 = bf16[192,8192]{1,0:T(8,128)(2,1)} collective-permute-done((bf16[192,8192]{1,0:T(8,128)(2,1)S(1)}, bf16[192,8192]{1,0:T(8,128)(2,1)}, u32[]{:S(2)}, u32[]{:S(2)}) %collective-permute-start.1) | collective-permute-done | bytes 3145760 | tf_op jit(solution)/shard_map/ppermute | solution.py:19
  157.7 3.9 all_to_all.27
  161.6 3.0 copy.38
  164.6 5.1 all-to-all-start.1
  171.3 90.7 %all-to-all-done.1 = bf16[192,4,1024]{2,0,1:T(8,128)(2,1)} async-done(((bf16[192,4,1024]{2,0,1:T(8,128)(2,1)}), bf16[192,4,1024]{2,0,1:T(8,128)(2,1)}, u32[]{:S(2)}, u32[]{:S(2)}) %all-to-all-start.1) | async-done | bytes 1572896 | tf_op jit(solution)/shard_map/all_to_all | solution.py:117
  276.8 8.3 %copy-done.2 = bf16[1536,8192]{1,0:T(8,128)(2,1)} copy-done((bf16[1536,8192]{1,0:T(8,128)(2,1)}, bf16[1536,8192]{1,0:T(8,128)(2,1)S(1)}, u32[]{:S(2)}) %copy-start.2) | copy-done | bytes 25165848
  285.1 4.8 fusion.81
  290.0 23.2 %fusion.66 = f32[768,1280]{0,1:T(8,128)S(1)} fusion(bf16[8192,1280]{1,0:T(8,128)(2,1)} %all-gather.2.cloned.1.call-done, bf16[1536,8192]{1,0:T(8,128)(2,1)} %copy-done.2, s32[]{:T(128)S(6)} %select_n.67), kind=kOutput, calls=%fused_computation.75 | convolution fusion | flops 16106127360 | bytes 37486596 | tf_op jit(solution)/shard_map/dot_general | solution.py:85
  321.8 3.7 add_convert_fusion
  328.2 90.0 %while.52 = (s32[]{:T(128)}, bf16[8,768,128]{2,1,0:T(8,128)(2,1)}, s32[8]{0:T(128)S(1)}, bf16[8,128,768]{2,1,0:T(8,128)(2,1)}, f32[8,768,768]{1,2,0:T(8,128)}, /...) while((s32[]{:T(128)}, bf16[8,768,128]{2,1,0:T(8,128)(2,1)}, ...), condition=%wide.region_5.6_spmd.clone, body=%wide.region_1.5_spmd.clone.sunk | while | flops 310344960 | bytes 20493544 | solution.py:76
  418.3 104.3 %while.53 = (s32[]{:T(128)}, bf16[768,8,128]{0,2,1:T(8,128)(2,1)S(1)}, bf16[768,1,128]{2,0,1:T(8,128)(2,1)}, s32[8]{0:T(128)S(1)}, bf16[8,768,128]{2,1,0:T(8,128...) while((s32[]{:T(128)}, ...), condition=%wide.region_9.10_spmd.clone, body=%wide.region_6.9_spmd.clone.sunk | while | flops 464683776 | bytes 17364168 | solution.py:76
  425.2 3.0 fusion.144
  438.2 3.0 fusion.144
  451.2 3.0 fusion.144
  477.3 3.0 fusion.144
  490.3 3.0 fusion.144
  516.3 3.0 fusion.144
  525.9 17.2 %psum.28 = bf16[768,32]{0,1:T(8,128)(2,1)S(1)} all-reduce(f32[768,32]{0,1:T(8,128)S(1)} %pad_maximum_fusion.2), channel_id=1, replica_groups=mesh['dp'=4,'fsdp'=2,'tensor'=4] {'tensor'}, use_global_device_ids=true, to_apply=%region_10.11 | all-reduce | flops 24576 | bytes 147456 | tf_op jit(solution)/shard_map/psum | solution.py:140
  543.1 9.3 %fusion.68 = f32[8192,32]{0,1:T(8,128)} fusion(bf16[1536,8192]{1,0:T(8,128)(2,1)} %copy-done.2, s32[]{:T(128)S(6)} %select_n.67, bf16[768,32]{0,1:T(8,128)(2,1)S(1)} %psum.28), kind=kOutput, calls=%fused_computation.77 | convolution fusion | flops 402915328 | bytes 13680644 | tf_op jit(solution)/shard_map/uh,ux->hx/dot_general | solution.py:141
  555.5 3.6 all-to-all-start
  559.2 14.2 %psum.31 = f32[16,128]{1,0:T(8,128)} all-reduce(f32[16,128]{1,0:T(8,128)S(1)} %convolution_multiply_fusion.2), channel_id=1, replica_groups=mesh['dp'=4,'fsdp'=2,'tensor'=4] {'dp','fsdp'}, use_global_device_ids=true, to_apply=%region_13.14 | all-reduce | flops 2048 | bytes 16384 | tf_op jit(solution)/shard_map/psum | solution.py:144
  573.4 35.4 %all-reduce.5.cloned.1.call-done = (f32[8192,32]{0,1:T(8,128)}, f32[16,1024]{1,0:T(8,128)}) async-done(((f32[8192,32]{0,1:T(8,128)}, f32[16,1024]{1,0:T(8,128)}), (f32[8192,32]{0,1:T(8,128)}, f32[16,1024]{1,0:T(8,128)})) %all-reduce.5.cloned.1.call-update) | async-done | bytes 1114128 | tf_op jit(solution)/shard_map/psum | solution.py:144
  (283 shorter events, 206.4 us)
Async XLA Ops:
  7.2 314.6 %copy-start = (bf16[16,1024]{1,0:T(8,128)(2,1)S(1)}, bf16[16,1024]{1,0:T(8,128)(2,1)}, u32[]{:S(2)}) copy-start(bf16[16,1024]{1,0:T(8,128)(2,1)} %param.16) | copy-start | bytes 98308
  7.2 3.6 copy-start.1
  7.2 3.6 copy-start.11
  7.2 282.8 %all-gather.2.cloned.1.call-start = ((), (), s32[]{:S(2)}) async-start(), calls=%async_computation.2 | async-start | bytes 23592960 | tf_op jit(solution)/shard_map/all_gather | solution.py:87
  11.6 73.2 %collective-permute-start = (bf16[192,8192]{1,0:T(8,128)(2,1)S(1)}, bf16[192,8192]{1,0:T(8,128)(2,1)S(1)}, u32[]{:S(2)}, u32[]{:S(2)}) collective-permute-start(bf16[192,8192]{1,0:T(8,128)(2,1)S(1)} %fusion.73), channel_id=1, source_target_pairs={{0,1},{1,2},{2,3},{3,0},{4,5},{5,6},{6,7},{7,4},{8,9},{9,10},{10,1... | collective-permute-start | bytes 9437192 | tf_op jit(solution)/shard_map/ppermute | solution.py:19
  84.9 1.7 copy-start.3
  86.6 71.2 %collective-permute-start.1 = (bf16[192,8192]{1,0:T(8,128)(2,1)S(1)}, bf16[192,8192]{1,0:T(8,128)(2,1)}, u32[]{:S(2)}, u32[]{:S(2)}) collective-permute-start(bf16[192,8192]{1,0:T(8,128)(2,1)S(1)} %collective-permute-done), channel_id=1, source_target_pairs={{0,1},{1,2},{2,3},{3,0},{4,5},{5,6},{6,7},{7,4},{8,9},{9,10},{10,1... | collective-permute-start | bytes 9437192 | tf_op jit(solution)/shard_map/ppermute | solution.py:19
  157.7 107.5 %collective-permute-start.2 = (bf16[192,8192]{1,0:T(8,128)(2,1)}, bf16[192,8192]{1,0:T(8,128)(2,1)}, u32[]{:S(2)}, u32[]{:S(2)}) collective-permute-start(bf16[192,8192]{1,0:T(8,128)(2,1)} %collective-permute-done.1), channel_id=1, source_target_pairs={{0,1},{1,2},{2,3},{3,0},{4,5},{5,6},{6,7},{7,4},{8,9},{9,10},{10,1... | collective-permute-start | bytes 9437192 | tf_op jit(solution)/shard_map/ppermute | solution.py:19
  164.6 97.3 %all-to-all-start.1 = ((bf16[192,4,1024]{2,0,1:T(8,128)(2,1)}), bf16[192,4,1024]{2,0,1:T(8,128)(2,1)}, u32[]{:S(2)}, u32[]{:S(2)}) async-start(bf16[192,4,1024]{2,0,1:T(8,128)(2,1)} %copy.38), calls=%async_computation.1 | async-start | bytes 3145728 | tf_op jit(solution)/shard_map/all_to_all | solution.py:117
  169.7 439.2 %all-reduce.5.cloned.1.call-start = ((), (), s32[]{:S(2)}) async-start(), calls=%async_computation.3 | async-start | bytes 2228224 | tf_op jit(solution)/shard_map/psum | solution.py:144
  267.3 2.8 copy-start.4
  276.8 8.3 %copy-start.2 = (bf16[1536,8192]{1,0:T(8,128)(2,1)}, bf16[1536,8192]{1,0:T(8,128)(2,1)S(1)}, u32[]{:S(2)}) copy-start(bf16[1536,8192]{1,0:T(8,128)(2,1)S(1)} %constant_dynamic-update-slice_fusion.1) | copy-start | bytes 75497472
  325.5 1.8 copy-start.8
  325.5 1.8 copy-start.13
  325.5 2.1 copy-start.10
  325.5 2.1 copy-start.5
  522.7 0.9 copy-start.6
  524.2 1.5 copy-start.9
  543.1 9.3 %copy-start.7 = (bf16[8,768,128]{2,1,0:T(8,128)(2,1)S(1)}, bf16[8,768,128]{2,1,0:T(8,128)(2,1)}, u32[]{:S(2)}) copy-start(bf16[8,768,128]{2,1,0:T(8,128)(2,1)} %get-tuple-element.648) | copy-start | bytes 4718596
  555.5 55.6 %all-to-all-start = ((bf16[4,192,1024]{2,1,0:T(8,128)(2,1)}), bf16[4,192,1024]{2,1,0:T(8,128)(2,1)S(1)}, u32[]{:S(2)}, u32[]{:S(2)}) async-start(bf16[4,192,1024]{2,1,0:T(8,128)(2,1)} %all_to_all.24), calls=%async_computation | async-start | bytes 3145728 | tf_op jit(solution)/shard_map/all_to_all | solution.py:120
  612.3 2.4 copy-start.12
Sparse Core Ops, SparseCore 0:
  9.9 110.1 all-gather.1
  552.5 56.2 all-reduce.4
